TPU v7x, 32 devices: a whole 2x2x4 slice. The times are simulated.
32 devices in a mesh: local: 4 (over z), data: 8 (over y, x, core).
Axes of the slice: x: 2, y: 2, z: 4, core: 2. Of those that a mesh axis runs over, the one named last changes fastest.
Arguments:
- tokens: bfloat16 [65536, 1024], P(('local', 'data'))
- grad_out: bfloat16 [65536, 1024], P(('local', 'data'))
- w_up: bfloat16 [2, 1024, 4096], P(None, ('local', 'data'))
- w_down: bfloat16 [2, 4096, 1024], P(None, ('local', 'data'))
Outputs:
- output 1: bfloat16 [65536, 1024], P(('local', 'data'))
- output 2: bfloat16 [65536, 1024], P(('local', 'data'))
- output 3: float32 [2, 1024, 4096], P(None, ('local', 'data'))
- output 4: float32 [2, 4096, 1024], P(None, ('local', 'data'))
All inputs are finite; a program needn't handle non-finite values.
Results may differ from a plain program's by a relative error of at most 0.0139185.
Values are sent between devices in bfloat16 or wider.
A program may use at most 1 GiB of HBM per device.

v0:
```python
import jax
import jax.numpy as jnp
from jax import lax
from jax.sharding import PartitionSpec as P

NORM_EPS = 1e-6
BOTH_AXES = ('local', 'data')
CONTRACT_ROWS = (((0,), (0,)), ((), ()))
CONTRACT_COLS = (((1,), (1,)), ((), ()))


def rms_norm(x_f32):
    return x_f32 * lax.rsqrt(jnp.mean(x_f32 * x_f32, axis=-1, keepdims=True) + NORM_EPS)


def gelu_tanh(values):
    return jax.nn.gelu(values, approximate=True)


def solution(mesh):
    n_local = mesh.shape['local']
    tok_spec = P(BOTH_AXES, None)
    w_spec = P(None, BOTH_AXES, None)

    def device_fn(tokens, grad_out, w_up, w_down):
        num_layers = w_up.shape[0]
        loc_index = lax.axis_index('local')
        saved_acts = []
        hidden_state = tokens
        for layer_idx in range(num_layers):
            up_full = lax.all_gather(w_up[layer_idx], BOTH_AXES, axis=0, tiled=True)
            down_full = lax.all_gather(w_down[layer_idx], BOTH_AXES, axis=0, tiled=True)
            up_rows = up_full.shape[0] // n_local
            down_rows = down_full.shape[0] // n_local
            up_second = lax.dynamic_slice_in_dim(up_full, loc_index * up_rows, up_rows, axis=0)
            down_second = lax.dynamic_slice_in_dim(down_full, loc_index * down_rows, down_rows, axis=0)
            x_f32 = hidden_state.astype(jnp.float32)
            normed = rms_norm(x_f32).astype(jnp.bfloat16)
            pre_act = jnp.dot(normed, up_full, preferred_element_type=jnp.float32).astype(jnp.bfloat16)
            hidden = gelu_tanh(pre_act.astype(jnp.float32)).astype(jnp.bfloat16)
            saved_acts.append((hidden_state, normed, pre_act, hidden, up_second, down_second))
            hidden_state = (x_f32 + jnp.dot(hidden, down_full, preferred_element_type=jnp.float32)).astype(jnp.bfloat16)
        cotangent = grad_out
        grads_up = [None] * num_layers
        grads_down = [None] * num_layers
        for layer_idx in reversed(range(num_layers)):
            layer_in, normed, pre_act, hidden, up_second, down_second = saved_acts[layer_idx]
            up_full = lax.all_gather(up_second, 'local', axis=0, tiled=True)
            down_full = lax.all_gather(down_second, 'local', axis=0, tiled=True)
            down_part = lax.dot_general(hidden, cotangent, CONTRACT_ROWS, preferred_element_type=jnp.float32)
            d_hidden = lax.dot_general(cotangent, down_full, CONTRACT_COLS, preferred_element_type=jnp.float32).astype(jnp.bfloat16)
            _, gelu_back = jax.vjp(gelu_tanh, pre_act.astype(jnp.float32))
            d_pre = gelu_back(d_hidden.astype(jnp.float32))[0].astype(jnp.bfloat16)
            up_part = lax.dot_general(normed, d_pre, CONTRACT_ROWS, preferred_element_type=jnp.float32)
            d_normed = lax.dot_general(d_pre, up_full, CONTRACT_COLS, preferred_element_type=jnp.float32)
            _, norm_back = jax.vjp(rms_norm, layer_in.astype(jnp.float32))
            cotangent = (cotangent.astype(jnp.float32) + norm_back(d_normed)[0]).astype(jnp.bfloat16)
            grads_up[layer_idx] = lax.psum_scatter(up_part, BOTH_AXES, scatter_dimension=0, tiled=True)
            grads_down[layer_idx] = lax.psum_scatter(down_part, BOTH_AXES, scatter_dimension=0, tiled=True)
        return hidden_state, cotangent, jnp.stack(grads_up), jnp.stack(grads_down)

    return jax.shard_map(device_fn, mesh=mesh, in_specs=(tok_spec, tok_spec, w_spec, w_spec), out_specs=(tok_spec, tok_spec, w_spec, w_spec), check_vma=False)
```

profile of v0, /device:TPU:14, one launch (start us, length us, event | category | flops | bytes accessed | tf_op | source)
XLA Modules:
  0.0 1680.9 jit_solution(2002432260441527269)
XLA Ops:
  12.4 76.1 %all-gather.23.cloned.1.call-done = bf16[1,4096,1024]{2,1,0:T(8,128)(2,1)} async-done(((bf16[1,128,1024]{2,1,0:T(8,128)(2,1)}), bf16[1,4096,1024]{2,1,0:T(8,128)(2,1)}) %all-gather.23.cloned.1.call-update) | async-done | bytes 8388624 | tf_op jit(solution)/shard_map/all_gather | solution.py:32
  91.6 76.1 %all-gather.21.cloned.1.call-done = bf16[1,1024,4096]{2,1,0:T(8,128)(2,1)} async-done(((bf16[1,32,4096]{2,1,0:T(8,128)(2,1)}), bf16[1,1024,4096]{2,1,0:T(8,128)(2,1)}) %all-gather.21.cloned.1.call-update) | async-done | bytes 8388624 | tf_op jit(solution)/shard_map/all_gather | solution.py:31
  167.7 3.2 constant_dynamic-slice_fusion.2
  170.9 76.0 %all-gather.19.cloned.1.call-done = bf16[1,4096,1024]{2,1,0:T(8,128)(2,1)} async-done(((bf16[1,128,1024]{2,1,0:T(8,128)(2,1)}), bf16[1,4096,1024]{2,1,0:T(8,128)(2,1)}) %all-gather.19.cloned.1.call-update) | async-done | bytes 8388624 | tf_op jit(solution)/shard_map/all_gather | solution.py:32
  247.0 3.1 constant_dynamic-slice_fusion.1
  250.1 6.4 copy.8
  260.3 65.8 %all-gather.17.cloned.1.call-done = bf16[1,1024,4096]{2,1,0:T(8,128)(2,1)} async-done(((bf16[1,32,4096]{2,1,0:T(8,128)(2,1)}), bf16[1,1024,4096]{2,1,0:T(8,128)(2,1)}) %all-gather.17.cloned.1.call-update) | async-done | bytes 8388624 | tf_op jit(solution)/shard_map/all_gather | solution.py:31
  326.1 25.3 %convolution_convert_fusion.1 = bf16[2048,4096]{1,0:T(8,128)(2,1)} fusion(bf16[1,1024,4096]{2,1,0:T(8,128)(2,1)} %all-gather.17.cloned.1.call-done, bf16[2048,1024]{0,1:T(8,128)(2,1)} %copy.8, f32[2048]{0:T(1024)S(1)} %fusion.56), kind=kOutput, calls=%fused_computation.45 | convolution fusion | flops 17194549248 | bytes 29368320 | tf_op jit(solution)/shard_map/dot_general | solution.py:39
  351.4 25.4 %fusion.30 = (f32[2048]{0:T(1024)S(1)}, bf16[2048,1024]{0,1:T(8,128)(2,1)}) fusion(bf16[1,4096,1024]{2,1,0:T(8,128)(2,1)} %all-gather.19.cloned.1.call-done, bf16[2048,4096]{1,0:T(8,128)(2,1)} %convolution_convert_fusion.1, bf16[2048,1024]{0,1:T(8,128)(2,1)S(1)} %copy-done), kind=kOutput, calls=%fused_computation.56 | convolution fusion | flops 17276336128 | bytes 33562624 | tf_op jit(solution)/shard_map/dot_general | solution.py:42
  377.4 3.2 constant_dynamic-slice_fusion
  380.7 25.2 %convolution_convert_fusion = bf16[2048,4096]{1,0:T(8,128)(2,1)} fusion(bf16[1,1024,4096]{2,1,0:T(8,128)(2,1)} %all-gather.21.cloned.1.call-done, bf16[2048,1024]{0,1:T(8,128)(2,1)} %get-tuple-element.13, f32[2048]{0:T(1024)S(1)} %fusion.57), kind=kOutput, calls=%fused_computation.44 | convolution fusion | flops 17194549248 | bytes 29368320 | tf_op jit(solution)/shard_map/dot_general | solution.py:39
  405.8 68.3 %all-gather.25.cloned.1.call-done = bf16[1,4096,1024]{2,1,0:T(8,128)(2,1)} async-done(((bf16[1,1024,1024]{2,1,0:T(8,128)(2,1)}), bf16[1,4096,1024]{2,1,0:T(8,128)(2,1)}) %all-gather.25.cloned.1.call-update) | async-done | bytes 8388624 | tf_op jit(solution)/shard_map/all_gather | solution.py:49
  474.2 44.4 %fusion.7 = bf16[2048,4096]{1,0:T(8,128)(2,1)} fusion(bf16[2048,4096]{1,0:T(8,128)(2,1)} %convolution_convert_fusion, bf16[2048,1024]{1,0:T(8,128)(2,1)} %param.5, bf16[1,4096,1024]{2,1,0:T(8,128)(2,1)} %all-gather.25.cloned.1.call-done), kind=kOutput, calls=%fused_computation.18 | convolution fusion | flops 17372807168 | bytes 46137344 | tf_op jit(solution)/shard_map/dot_general | solution.py:51
  518.6 22.6 %fusion.50 = f32[1024,4096]{1,0:T(8,128)} fusion(bf16[2048,4096]{1,0:T(8,128)(2,1)} %fusion.7, bf16[2048,1024]{0,1:T(8,128)(2,1)S(1)} %copy-done.5, f32[2048]{0:T(1024)S(1)} %fusion.57), kind=kOutput, calls=%fused_computation.72 | convolution fusion | flops 17186160640 | bytes 37756928 | tf_op jit(solution)/shard_map/dot_general | solution.py:54
  541.3 6.5 copy.10
  547.8 75.7 %all-gather.27.cloned.1.call-done = bf16[1,1024,4096]{2,1,0:T(8,128)(2,1)} async-done(((bf16[1,256,4096]{2,1,0:T(8,128)(2,1)}), bf16[1,1024,4096]{2,1,0:T(8,128)(2,1)}) %all-gather.27.cloned.1.call-update) | async-done | bytes 8388624 | tf_op jit(solution)/shard_map/all_gather | solution.py:48
  623.6 23.3 %fusion.33 = (f32[2048]{0:T(1024)S(1)}, f32[2048,1024]{0,1:T(8,128)S(1)}) fusion(bf16[2048,1024]{0,1:T(8,128)(2,1)} %get-tuple-element.13, bf16[2048,4096]{1,0:T(8,128)(2,1)} %fusion.7, bf16[1,1024,4096]{2,1,0:T(8,128)(2,1)} %all-gather.27.cloned.1.call-done), kind=kOutput, calls=%fused_computation.59 | convolution fusion | flops 17186158592 | bytes 37756928 | tf_op jit(solution)/shard_map/dot_general | solution.py:55
  646.9 4.0 fusion.23
  651.0 122.1 %all-gather.29.cloned.1.call-done = bf16[1,4096,1024]{2,1,0:T(8,128)(2,1)} async-done(((bf16[1,1024,1024]{2,1,0:T(8,128)(2,1)}), bf16[1,4096,1024]{2,1,0:T(8,128)(2,1)}) %all-gather.29.cloned.1.call-update) | async-done | bytes 8388624 | tf_op jit(solution)/shard_map/all_gather | solution.py:49
  773.1 48.7 %fusion.4 = bf16[2048,4096]{1,0:T(8,128)(2,1)} fusion(bf16[2048,4096]{1,0:T(8,128)(2,1)} %convolution_convert_fusion.1, bf16[2048,1024]{0,1:T(8,128)(2,1)} %fusion.23, bf16[1,4096,1024]{2,1,0:T(8,128)(2,1)} %all-gather.29.cloned.1.call-done), kind=kOutput, calls=%fused_computation.15 | convolution fusion | flops 17372807168 | bytes 46137344 | tf_op jit(solution)/shard_map/dot_general | solution.py:51
  821.7 22.5 %fusion.53 = f32[1024,4096]{1,0:T(8,128)} fusion(bf16[2048,4096]{1,0:T(8,128)(2,1)} %fusion.4, bf16[2048,1024]{0,1:T(8,128)(2,1)S(1)} %copy-done.1, f32[2048]{0:T(1024)S(1)} %copy-done.10), kind=kOutput, calls=%fused_computation.73 | convolution fusion | flops 17186160640 | bytes 37756928 | tf_op jit(solution)/shard_map/dot_general | solution.py:54
  844.3 28.9 %fusion.58 = f32[4096,1024]{1,0:T(8,128)} fusion(bf16[2048,1024]{1,0:T(8,128)(2,1)} %param.5, bf16[2048,4096]{1,0:T(8,128)(2,1)} %convolution_convert_fusion), kind=kOutput, calls=%fused_computation.86 | convolution fusion | flops 17263755264 | bytes 37748736 | tf_op jit(solution)/shard_map/dot_general | solution.py:50
  873.3 29.3 %fusion.61 = f32[4096,1024]{1,0:T(8,128)} fusion(bf16[2048,1024]{0,1:T(8,128)(2,1)} %fusion.23, bf16[2048,4096]{1,0:T(8,128)(2,1)} %convolution_convert_fusion.1), kind=kOutput, calls=%fused_computation.87 | convolution fusion | flops 17263755264 | bytes 37748736 | tf_op jit(solution)/shard_map/dot_general | solution.py:50
  902.6 25.2 %fusion.32 = bf16[2048,1024]{0,1:T(8,128)(2,1)} fusion(bf16[2048,1024]{0,1:T(8,128)(2,1)} %get-tuple-element.13, bf16[1,4096,1024]{2,1,0:T(8,128)(2,1)} %all-gather.23.cloned.1.call-done, bf16[2048,4096]{1,0:T(8,128)(2,1)} %convolution_convert_fusion), kind=kOutput, calls=%fused_computation.58 | convolution fusion | flops 17270046720 | bytes 33554432 | tf_op jit(solution)/shard_map/dot_general | solution.py:42
  927.8 6.4 copy.12
  934.2 23.6 %fusion.29 = (f32[2048]{0:T(1024)S(1)}, f32[2048,1024]{0,1:T(8,128)S(1)}) fusion(bf16[2048,1024]{0,1:T(8,128)(2,1)} %copy.8, bf16[2048,4096]{1,0:T(8,128)(2,1)} %fusion.4, bf16[1,1024,4096]{2,1,0:T(8,128)(2,1)} %all-gather.31.cloned.1.call-done), kind=kOutput, calls=%fused_computation.55 | convolution fusion | flops 17186158592 | bytes 37756928 | tf_op jit(solution)/shard_map/dot_general | solution.py:55
  958.0 4.1 fusion.25
  962.0 6.4 copy.13
  968.4 142.6 %reduce-scatter.7.cloned.1.call-done = f32[32,4096]{1,0:T(8,128)} async-done(((f32[1024,4096]{1,0:T(8,128)}), f32[32,4096]{1,0:T(8,128)}) %reduce-scatter.7.cloned.1.call-update) | async-done | bytes 524304 | tf_op jit(solution)/shard_map/reduce_scatter | solution.py:58
  1111.1 186.7 %reduce-scatter.5.cloned.1.call-done = f32[32,4096]{1,0:T(8,128)} async-done(((f32[1024,4096]{1,0:T(8,128)}), f32[32,4096]{1,0:T(8,128)}) %reduce-scatter.5.cloned.1.call-update) | async-done | bytes 524304 | tf_op jit(solution)/shard_map/reduce_scatter | solution.py:58
  1300.0 184.6 %reduce-scatter.11.cloned.1.call-done = f32[128,1024]{1,0:T(8,128)} async-done(((f32[4096,1024]{1,0:T(8,128)}), f32[128,1024]{1,0:T(8,128)}) %reduce-scatter.11.cloned.1.call-update) | async-done | bytes 524304 | tf_op jit(solution)/shard_map/reduce_scatter | solution.py:59
  1484.6 186.7 %reduce-scatter.9.cloned.1.call-done = f32[128,1024]{1,0:T(8,128)} async-done(((f32[4096,1024]{1,0:T(8,128)}), f32[128,1024]{1,0:T(8,128)}) %reduce-scatter.9.cloned.1.call-update) | async-done | bytes 524304 | tf_op jit(solution)/shard_map/reduce_scatter | solution.py:59
  (63 shorter events, 17.5 us)
Async XLA Ops:
  7.2 81.3 %all-gather.23.cloned.1.call-start = ((), (), s32[]{:S(2)}) async-start(), calls=%async_computation.11 | async-start | bytes 8650752 | tf_op jit(solution)/shard_map/all_gather | solution.py:32
  9.1 158.6 %all-gather.21.cloned.1.call-start = ((), (), s32[]{:S(2)}) async-start(), calls=%async_computation.10 | async-start | bytes 8650752 | tf_op jit(solution)/shard_map/all_gather | solution.py:31
  11.0 235.9 %all-gather.19.cloned.1.call-start = ((), (), s32[]{:S(2)}) async-start(), calls=%async_computation.9 | async-start | bytes 8650752 | tf_op jit(solution)/shard_map/all_gather | solution.py:32
  11.8 314.3 %all-gather.17.cloned.1.call-start = ((), (), s32[]{:S(2)}) async-start(), calls=%async_computation.8 | async-start | bytes 8650752 | tf_op jit(solution)/shard_map/all_gather | solution.py:31
  12.3 461.8 %all-gather.25.cloned.1.call-start = ((), (), s32[]{:S(2)}) async-start(), calls=%async_computation.12 | async-start | bytes 10485760 | tf_op jit(solution)/shard_map/all_gather | solution.py:49
  91.5 532.0 %all-gather.27.cloned.1.call-start = ((), (), s32[]{:S(2)}) async-start(), calls=%async_computation.13 | async-start | bytes 10485760 | tf_op jit(solution)/shard_map/all_gather | solution.py:48
  170.9 602.2 %all-gather.29.cloned.1.call-start = ((), (), s32[]{:S(2)}) async-start(), calls=%async_computation.14 | async-start | bytes 10485760 | tf_op jit(solution)/shard_map/all_gather | solution.py:49
  250.1 684.1 %all-gather.31.cloned.1.call-start = ((), (), s32[]{:S(2)}) async-start(), calls=%async_computation.15 | async-start | bytes 10485760 | tf_op jit(solution)/shard_map/all_gather | solution.py:48
  259.6 0.6 copy-start.7
  260.3 91.1 %copy-start.9 = (f32[2048]{0:T(1024)}, f32[2048]{0:T(1024)S(1)}, u32[]{:S(2)}) copy-start(f32[2048]{0:T(1024)S(1)} %fusion.56) | copy-start | bytes 24580
  326.1 25.3 %copy-start = (bf16[2048,1024]{0,1:T(8,128)(2,1)S(1)}, bf16[2048,1024]{0,1:T(8,128)(2,1)}, u32[]{:S(2)}) copy-start(bf16[2048,1024]{0,1:T(8,128)(2,1)} %copy.8) | copy-start | bytes 12582916
  376.8 0.6 copy-start.12
  380.6 730.4 %reduce-scatter.7.cloned.1.call-start = ((), (), s32[]{:S(2)}) async-start(), calls=%async_computation.5 | async-start | bytes 17301504 | tf_op jit(solution)/shard_map/reduce_scatter | solution.py:58
  474.2 44.4 %copy-start.5 = (bf16[2048,1024]{0,1:T(8,128)(2,1)S(1)}, bf16[2048,1024]{0,1:T(8,128)(2,1)}, u32[]{:S(2)}) copy-start(bf16[2048,1024]{0,1:T(8,128)(2,1)} %get-tuple-element.13) | copy-start | bytes 12582916
  541.3 756.5 %reduce-scatter.5.cloned.1.call-start = ((), (), s32[]{:S(2)}) async-start(), calls=%async_computation.4 | async-start | bytes 17301504 | tf_op jit(solution)/shard_map/reduce_scatter | solution.py:58
  547.8 99.0 %copy-start.13 = (f32[2048]{0:T(1024)S(1)}, f32[2048]{0:T(1024)}, u32[]{:S(2)}) copy-start(f32[2048]{0:T(1024)} %copy-done.12) | copy-start | bytes 24580
  623.5 23.4 %copy-start.3 = (bf16[2048,1024]{0,1:T(8,128)(2,1)S(1)}, bf16[2048,1024]{0,1:T(8,128)(2,1)}, u32[]{:S(2)}) copy-start(bf16[2048,1024]{0,1:T(8,128)(2,1)} %copy.10) | copy-start | bytes 12582916
  623.5 23.4 %copy-start.6 = (bf16[2048,1024]{0,1:T(8,128)(2,1)S(1)}, bf16[2048,1024]{0,1:T(8,128)(2,1)}, u32[]{:S(2)}) copy-start(bf16[2048,1024]{0,1:T(8,128)(2,1)} %get-tuple-element.13) | copy-start | bytes 12582916
  651.0 170.8 %copy-start.10 = (f32[2048]{0:T(1024)S(1)}, f32[2048]{0:T(1024)}, u32[]{:S(2)}) copy-start(f32[2048]{0:T(1024)} %copy-done.9) | copy-start | bytes 24580
  773.1 48.7 %copy-start.1 = (bf16[2048,1024]{0,1:T(8,128)(2,1)S(1)}, bf16[2048,1024]{0,1:T(8,128)(2,1)}, u32[]{:S(2)}) copy-start(bf16[2048,1024]{0,1:T(8,128)(2,1)} %copy.8) | copy-start | bytes 12582916
  844.3 640.3 %reduce-scatter.11.cloned.1.call-start = ((), (), s32[]{:S(2)}) async-start(), calls=%async_computation.7 | async-start | bytes 17301504 | tf_op jit(solution)/shard_map/reduce_scatter | solution.py:59
  873.3 798.0 %reduce-scatter.9.cloned.1.call-start = ((), (), s32[]{:S(2)}) async-start(), calls=%async_computation.6 | async-start | bytes 17301504 | tf_op jit(solution)/shard_map/reduce_scatter | solution.py:59
  934.2 23.7 %copy-start.8 = (f32[2048]{0:T(1024)S(1)}, f32[2048]{0:T(1024)}, u32[]{:S(2)}) copy-start(f32[2048]{0:T(1024)} %copy-done.7) | copy-start | bytes 24580
  934.2 23.7 %copy-start.11 = (f32[2048]{0:T(1024)S(1)}, f32[2048]{0:T(1024)}, u32[]{:S(2)}) copy-start(f32[2048]{0:T(1024)} %copy-done.9) | copy-start | bytes 24580
  934.2 23.7 %copy-start.2 = (bf16[2048,1024]{0,1:T(8,128)(2,1)S(1)}, bf16[2048,1024]{0,1:T(8,128)(2,1)}, u32[]{:S(2)}) copy-start(bf16[2048,1024]{0,1:T(8,128)(2,1)} %copy.8) | copy-start | bytes 12582916
  934.2 23.7 %copy-start.4 = (bf16[2048,1024]{0,1:T(8,128)(2,1)S(1)}, bf16[2048,1024]{0,1:T(8,128)(2,1)}, u32[]{:S(2)}) copy-start(bf16[2048,1024]{0,1:T(8,128)(2,1)} %fusion.23) | copy-start | bytes 12582916
Sparse Core Ops, SparseCore 0:
  11.4 76.9 all-gather.22
  91.9 75.7 all-gather.20
  171.1 75.7 all-gather.18
  250.3 75.7 all-gather.16
  327.5 146.6 all-gather.24
  475.6 147.8 all-gather.26
  625.1 147.8 all-gather.28
  774.6 147.8 all-gather.30
  924.9 186.1 reduce-scatter.6
  1113.2 184.5 reduce-scatter.4
  1300.1 184.5 reduce-scatter.10
  1486.8 184.5 reduce-scatter.8
where the time goes:
time: 1690 us; the launch traced here: 1680 us
  waiting for transfers between devices  1260 us (75%)
  matrix products  345 us (20%)
  local copies, waits for them, and re-layouts  43.2 us (3%)
    reduce_scatter x2, waiting for transfers between devices, device_fn(): lax.psum_scatter(down_part, BOTH_AXES, scatter_dimension=0, tiled=True)  371 us
    reduce_scatter x2, waiting for transfers between devices, device_fn(): lax.psum_scatter(up_part, BOTH_AXES, scatter_dimension=0, tiled=True)  329 us
    all_gather x2, waiting for transfers between devices, device_fn(): down_full = lax.all_gather(down_second, 'local', axis=0, tiled=True)  190 us
    all_gather x2, waiting for transfers between devices, device_fn(): down_full = lax.all_gather(w_down[layer_idx], BOTH_AXES, axis=0, tiled=True)  152 us
    all_gather x2, waiting for transfers between devices, device_fn(): up_full = lax.all_gather(w_up[layer_idx], BOTH_AXES, axis=0, tiled=True)  142 us
    dot_general x2, matrix products, device_fn(): lax.dot_general(cotangent, down_full, CONTRACT_COLS, preferred_element_ty...  93.1 us
    all_gather x2, waiting for transfers between devices, device_fn(): up_full = lax.all_gather(up_second, 'local', axis=0, tiled=True)  75.7 us
    dot_general x2, matrix products, device_fn(): lax.dot_general(hidden, cotangent, CONTRACT_ROWS, preferred_element_type=...  58.2 us
  transfers between devices with their start and end apart: 12, of which 11 were waited for; matrix products, arithmetic and copies ran while one was open for 24% of the time, Pallas kernels for 0%

commit v1 on v0

v1 whole, which is shorter than its diff:
```python
import functools

import jax
import jax.numpy as jnp
from jax import lax
from jax.experimental import pallas as pl
from jax.experimental.pallas import tpu as pltpu
from jax.sharding import PartitionSpec as P

NORM_EPS = 1e-6
BOTH_AXES = ('local', 'data')
CONTRACT_ROWS = (((0,), (0,)), ((), ()))
CONTRACT_COLS = (((1,), (1,)), ((), ()))
TANH_SCALE = 0.7978845608028654
TANH_CUBIC = 0.044715
STEPS = 8
PARTS = 4
N_CHUNKS = 4
VMEM_LIMIT = 62 * 1024 * 1024
F32 = jnp.float32
BF16 = jnp.bfloat16
ANY = pl.BlockSpec(memory_space=pl.ANY)


class Place:

    def __init__(self):
        self.z = lax.axis_index('local')
        self.j = lax.axis_index('data')
        self.core = lax.rem(self.j, 2)
        self.x = lax.rem(lax.div(self.j, 2), 2)
        self.y = lax.div(self.j, 4)
        self.z1 = self.z + 1 - 2 * lax.rem(self.z, 2)
        self.z2 = lax.rem(self.z + 2, 4)
        self.z3 = 3 - self.z
        self.ja = self.plane(0, 1, self.core)
        self.jb = self.plane(1, 0, self.core)
        self.jab = self.plane(1, 1, self.core)
        self.jc = self.plane(0, 0, 1 - self.core)

    def plane(self, flip_b, flip_a, core):
        y_bit = flip_b + core * (flip_a - flip_b)
        x_bit = flip_a + core * (flip_b - flip_a)
        y = self.y + y_bit - 2 * self.y * y_bit
        x = self.x + x_bit - 2 * self.x * x_bit
        return y * 4 + x * 2 + core

    def peers(self):
        return [(self.z1, self.j), (self.z2, self.j), (self.z, self.ja), (self.z, self.jb), (self.z, self.jc)]


def greet(at):
    barrier = pltpu.get_barrier_semaphore()
    for peer in at.peers():
        pl.semaphore_signal(barrier, inc=1, device_id=peer, device_id_type=pl.DeviceIdType.MESH)
    pl.semaphore_wait(barrier, 5)


def remote(src, dst, sems, k, peer):
    return pltpu.make_async_remote_copy(
        src_ref=src, dst_ref=dst, send_sem=sems[0].at[k], recv_sem=sems[1].at[k],
        device_id=peer, device_id_type=pl.DeviceIdType.MESH)


def gather_scratch(shard):
    return [
        pltpu.VMEM(shard.shape, shard.dtype),
        pltpu.SemaphoreType.DMA((2,)),
        pltpu.SemaphoreType.DMA((10,)),
        pltpu.SemaphoreType.DMA((10,)),
    ]


def gather_actions(shard, full, buf, local_sems, send_sems, recv_sems):
    at = Place()
    sems = (send_sems, recv_sems)
    j = at.j
    to_z1, to_z2 = (at.z1, j), (at.z2, j)
    to_a, to_b, to_c = (at.z, at.ja), (at.z, at.jb), (at.z, at.jc)
    columns = (j, at.ja, at.jb, at.jab)

    def load():
        return pltpu.make_async_copy(shard, buf, local_sems.at[0])

    def store():
        return pltpu.make_async_copy(buf, full.at[at.z, j], local_sems.at[1])

    def hop(k):
        src, dst, peer = (
            (lambda: shard, lambda: full.at[at.z, j], to_z2),
            (lambda: shard, lambda: full.at[at.z, j], to_z1),
            (lambda: full.at[at.z2, j], lambda: full.at[at.z2, j], to_z1),
            (lambda: full.at[:, j], lambda: full.at[:, j], to_a),
            (lambda: full.at[:, j], lambda: full.at[:, j], to_b),
            (lambda: full.at[:, at.ja], lambda: full.at[:, at.ja], to_b),
        )[k]
        return remote(src(), dst(), sems, k, peer)

    def across(k):
        return remote(full.at[:, columns[k]], full.at[:, columns[k]], sems, 6 + k, to_c)

    def first():
        greet(at)
        load().start()
        hop(0).start()
        hop(1).start()
        load().wait()
        store().start()

    def second():
        hop(0).wait_recv()
        hop(2).start()

    def third():
        store().wait()
        hop(1).wait_recv()
        hop(2).wait_recv()
        hop(4).start()
        hop(3).start()
        across(0).start()

    def fourth():
        hop(3).wait_recv()
        hop(5).start()
        across(1).start()

    def fifth():
        hop(4).wait_recv()
        across(2).start()

    def sixth():
        hop(5).wait_recv()
        across(3).start()

    def last():
        for k in range(4):
            across(k).wait_recv()
        for k in range(6):
            hop(k).wait_send()
        for k in range(4):
            across(k).wait_send()

    return [first, second, third, fourth, fifth, sixth, last]


def scatter_scratch(part):
    _, _, n, m = part.shape
    w = m // N_CHUNKS
    q = N_CHUNKS
    return [
        pltpu.VMEM((q, 2, 2, 4, n, w), F32),
        pltpu.VMEM((q, 2, 2, 4, n, w), F32),
        pltpu.VMEM((q, 2, 4, n, w), F32),
        pltpu.VMEM((q, 4, n, w), F32),
        pltpu.VMEM((q, 2, n, w), F32),
        pltpu.VMEM((q, n, w), F32),
        pltpu.SemaphoreType.DMA((q * 4,)),
        pltpu.SemaphoreType.DMA((q * 9,)),
        pltpu.SemaphoreType.DMA((q * 9,)),
    ]


def scatter_actions(part, out, own, got_core, got_b, got_a, got_z1, got_z2, local_sems, send_sems, recv_sems):
    at = Place()
    sems = (send_sems, recv_sems)
    w = out.shape[1] // N_CHUNKS
    to_z1, to_z2 = (at.z1, at.j), (at.z2, at.j)
    to_a, to_b, to_c = (at.z, at.ja), (at.z, at.jb), (at.z, at.jc)

    def load(q, b, a):
        return pltpu.make_async_copy(
            part.at[:, at.plane(b, a, at.core), :, pl.ds(q * w, w)], own.at[q, b, a], local_sems.at[q * 4 + b * 2 + a])

    def swap(q, b, a):
        return remote(part.at[:, at.plane(b, a, 1 - at.core), :, pl.ds(q * w, w)], got_core.at[q, b, a], sems, q * 9 + b * 2 + a, to_c)

    def over_b(q):
        return remote(own.at[q, 1], got_b.at[q], sems, q * 9 + 4, to_b)

    def over_a(q):
        return remote(own.at[q, 0, 1], got_a.at[q], sems, q * 9 + 5, to_a)

    def over_z1(q, k):
        return remote(own.at[q, 0, 0, (at.z1, at.z3)[k]], got_z1.at[q, k], sems, q * 9 + 6 + k, to_z1)

    def over_z2(q):
        return remote(own.at[q, 0, 0, at.z2], got_z2.at[q], sems, q * 9 + 8, to_z2)

    def begin():
        greet(at)
        for b in (1, 0):
            for q in range(N_CHUNKS):
                for a in range(2):
                    swap(q, b, a).start()
                    load(q, b, a).start()

    def chip_far(q):
        for a in range(2):
            load(q, 1, a).wait()
            swap(q, 1, a).wait_recv()
            own[q, 1, a] += got_core[q, 1, a]
        over_b(q).start()

    def chip_near(q):
        for a in range(2):
            load(q, 0, a).wait()
            swap(q, 0, a).wait_recv()
            own[q, 0, a] += got_core[q, 0, a]

    def after_b(q):
        over_b(q).wait_recv()
        own[q, 0, 1] += got_b[q, 1]
        over_a(q).start()
        own[q, 0, 0] += got_b[q, 0]

    def after_a(q):
        over_a(q).wait_recv()
        own[q, 0, 0] += got_a[q]
        for k in range(2):
            over_z1(q, k).start()

    def after_z1(q):
        for k in range(2):
            over_z1(q, k).wait_recv()
        own[q, 0, 0, at.z2] += got_z1[q, 1]
        over_z2(q).start()

    def after_z2(q):
        over_z2(q).wait_recv()
        out[:, q * w:(q + 1) * w] = own[q, 0, 0, at.z] + got_z1[q, 0] + got_z2[q]

    def end():
        for q in range(N_CHUNKS):
            for b in range(2):
                for a in range(2):
                    swap(q, b, a).wait_send()
            over_b(q).wait_send()
            over_a(q).wait_send()
            for k in range(2):
                over_z1(q, k).wait_send()
            over_z2(q).wait_send()

    return begin, chip_far, chip_near, after_b, after_a, after_z1, after_z2, end


def scatter_plan(functions, slots):
    begin, chip_far, chip_near, after_b, after_a, after_z1, after_z2, end = functions
    plan = {slot: [] for slot in range(slots)}

    def put(slot, fn):
        plan[min(slot, slots - 1)].append((slot, len(plan[min(slot, slots - 1)]), fn))

    put(0, begin)
    for q in range(N_CHUNKS):
        part = functools.partial
        put(1 + q // 2, part(chip_far, q))
        put(3, part(chip_near, q))
        put(4 + 4 * q, part(after_b, q))
        put(7 + 4 * q, part(after_a, q))
        put(9 + 4 * q, part(after_z1, q))
        put(11 + 4 * q, part(after_z2, q))
    put(10_000, end)
    return {slot: [fn for _, _, fn in sorted(entries, key=lambda e: e[:2])] for slot, entries in plan.items()}


def norm_scale(x):
    return lax.rsqrt(jnp.mean(x * x, axis=-1, keepdims=True) + NORM_EPS)


def dot(lhs, rhs):
    return jnp.dot(lhs, rhs, preferred_element_type=F32)


def dot_cols(lhs, rhs):
    return lax.dot_general(lhs, rhs, CONTRACT_COLS, preferred_element_type=F32)


def enter_pieces(x_ref, w_ref, u_ref, a_ref, s_ref):
    width = w_ref.shape[1] // PARTS

    def piece(k):
        if k == 0:
            x = x_ref[...].astype(F32)
            u_ref[...] = (x * norm_scale(x)).astype(BF16)
        cols = slice(k * width, (k + 1) * width)
        pre = dot(u_ref[...], w_ref[:, cols]).astype(BF16)
        a_ref[:, cols] = pre
        a = pre.astype(F32)
        t = jnp.tanh(a * (TANH_SCALE + (TANH_SCALE * TANH_CUBIC) * (a * a)))
        s_ref[:, cols] = (0.5 * a * (1.0 + t)).astype(BF16)

    return [functools.partial(piece, k) for k in range(PARTS)]


def leave_pieces(s_ref, x_ref, w_ref, out_ref):
    width = out_ref.shape[1] // 2

    def piece(k):
        cols = slice(k * width, (k + 1) * width)
        out_ref[:, cols] = (x_ref[:, cols].astype(F32) + dot(s_ref[...], w_ref[:, cols])).astype(BF16)

    return [functools.partial(piece, k) for k in range(2)]


def back_hidden_pieces(dy_ref, a_ref, w_ref, da_ref):
    width = a_ref.shape[1] // PARTS

    def piece(k):
        cols = slice(k * width, (k + 1) * width)
        ds = dot_cols(dy_ref[...], w_ref[cols, :]).astype(BF16).astype(F32)
        a = a_ref[:, cols].astype(F32)
        sq = a * a
        t = jnp.tanh(a * (TANH_SCALE + (TANH_SCALE * TANH_CUBIC) * sq))
        slope = (0.5 + 0.5 * t) + (a * (1.0 - t * t)) * (0.5 * TANH_SCALE + (1.5 * TANH_SCALE * TANH_CUBIC) * sq)
        da_ref[:, cols] = (ds * slope).astype(BF16)

    return [functools.partial(piece, k) for k in range(PARTS)]


def back_hidden_leave_pieces(dy_ref, a_ref, s_ref, x_ref, w_ref, da_ref, out_ref):
    return back_hidden_pieces(dy_ref, a_ref, w_ref, da_ref) + leave_pieces(s_ref, x_ref, w_ref, out_ref)


def back_input_pieces(da_ref, x_ref, dy_ref, w_ref, dx_ref, du_ref):
    width = w_ref.shape[0] // 2

    def piece(k):
        cols = slice(k * width, (k + 1) * width)
        du_ref[:, cols] = dot_cols(da_ref[...], w_ref[cols, :])
        if k == 1:
            x = x_ref[...].astype(F32)
            r = norm_scale(x)
            xr = x * r
            du = du_ref[...]
            along = jnp.mean(xr * du, axis=-1, keepdims=True)
            dx_ref[...] = (dy_ref[...].astype(F32) + r * (du - xr * along)).astype(BF16)

    return [functools.partial(piece, k) for k in range(2)]


def run_steps(pieces, plan, per_step):
    step = pl.program_id(0)
    slots_per_step = per_step
    each = len(pieces) // slots_per_step
    slots = STEPS * slots_per_step
    for part in range(slots_per_step):
        for s in range(STEPS):
            fns = plan.get(s * slots_per_step + part, []) if s * slots_per_step + part < slots else []
            if fns:
                def act(fns=fns):
                    for fn in fns:
                        fn()
                pl.when(step == s)(act)
        for piece in pieces[part * each:(part + 1) * each]:
            piece()
    rest = [fn for slot in sorted(plan) if slot >= slots for fn in plan[slot]]
    if rest:
        def finish():
            for fn in rest:
                fn()
        pl.when(step == STEPS - 1)(finish)


def row_spec(array_shape):
    return pl.BlockSpec((array_shape[0] // STEPS, array_shape[1]), lambda i: (i, 0))


def whole_spec(shape):
    return pl.BlockSpec(shape, lambda i: (0,) * len(shape), pipeline_mode=pl.Buffered(1))


def fused_call(name, make_pieces, rows_in, weight, outs, comm, comm_in, collective_id, scratch=()):
    n_in, n_out, n_scratch = len(rows_in) + 1, len(outs), len(scratch)
    per_step = 2
    out_shape = [jax.ShapeDtypeStruct(shape, dtype) for shape, dtype in outs]
    out_specs = [row_spec(shape) for shape, _ in outs]
    scratch_shapes = list(scratch)
    if comm == 'gather':
        n, m = comm_in.shape
        out_shape.append(jax.ShapeDtypeStruct((4, 8, n, m), comm_in.dtype))
        out_specs.append(ANY)
        scratch_shapes += gather_scratch(comm_in)
    else:
        _, _, n, m = comm_in.shape
        out_shape.append(jax.ShapeDtypeStruct((n, m), F32))
        out_specs.append(pl.BlockSpec((n, m), lambda i: (0, 0)))
        scratch_shapes += scatter_scratch(comm_in)

    def kernel(*refs):
        ins, comm_ref = refs[:n_in], refs[n_in]
        out_refs, comm_out = refs[n_in + 1:n_in + 1 + n_out], refs[n_in + 1 + n_out]
        rest = refs[n_in + 2 + n_out:]
        own, comm_scratch = rest[:n_scratch], rest[n_scratch:]
        if comm == 'gather':
            acts = gather_actions(comm_ref, comm_out, *comm_scratch)
            slots = (0, 2, 4, 8, 9, 13, 10_000)
            plan = {slot: [fn] for slot, fn in zip(slots, acts)}
        else:
            functions = scatter_actions(comm_ref, comm_out, *comm_scratch)
            plan = scatter_plan(functions, STEPS * per_step + 1)
        run_steps(make_pieces(*ins, *out_refs, *own), plan, per_step)

    rows = rows_in[0].shape[0]
    flops = 2 * rows * weight.size
    result = pl.pallas_call(
        kernel,
        grid=(STEPS,),
        out_shape=out_shape,
        in_specs=[row_spec(v.shape) for v in rows_in] + [whole_spec(weight.shape), ANY],
        out_specs=out_specs,
        scratch_shapes=scratch_shapes,
        compiler_params=pltpu.CompilerParams(
            dimension_semantics=('arbitrary',), collective_id=collective_id, has_side_effects=True, vmem_limit_bytes=VMEM_LIMIT),
        cost_estimate=pl.CostEstimate(flops=2 * flops, bytes_accessed=64 << 20, transcendentals=0),
        name=name,
    )(*rows_in, weight, comm_in)
    if comm == 'gather':
        result = [*result[:-1], result[-1].reshape(32 * comm_in.shape[0], comm_in.shape[1])]
    return result


def gather_alone(shard, collective_id):
    n, m = shard.shape

    def kernel(shard_ref, full_ref, *scratch):
        for fn in gather_actions(shard_ref, full_ref, *scratch):
            fn()

    full = pl.pallas_call(
        kernel,
        out_shape=jax.ShapeDtypeStruct((4, 8, n, m), shard.dtype),
        in_specs=[ANY],
        out_specs=ANY,
        scratch_shapes=gather_scratch(shard),
        compiler_params=pltpu.CompilerParams(collective_id=collective_id, has_side_effects=True, vmem_limit_bytes=VMEM_LIMIT),
        cost_estimate=pl.CostEstimate(flops=1 << 34, bytes_accessed=16 << 20, transcendentals=0),
        name='gather_alone',
    )(shard)
    return full.reshape(32 * n, m)


def solution(mesh):
    tok_spec = P(BOTH_AXES, None)
    w_spec = P(None, BOTH_AXES, None)

    def device_fn(tokens, grad_out, w_up, w_down):
        t, d = tokens.shape
        f = w_up.shape[2]
        wide, narrow = ((t, f), BF16), ((t, d), BF16)

        def again(shard, value):
            shard, _ = lax.optimization_barrier((shard, value))
            return lax.all_gather(shard, BOTH_AXES, axis=0, tiled=True)

        def grad(lhs, rhs):
            part = lax.dot_general(lhs, rhs, CONTRACT_ROWS, preferred_element_type=F32)
            return part.reshape(4, 8, part.shape[0] // 32, part.shape[1])

        up0 = gather_alone(w_up[0], 0)
        u0, a0, s0, down0 = fused_call('enter_0', enter_pieces, [tokens], up0, [narrow, wide, wide], 'gather', w_down[0], 1)
        mid, up1 = fused_call('leave_0', leave_pieces, [s0, tokens], down0, [narrow], 'gather', w_up[1], 2)
        u1, a1, s1, down1 = fused_call('enter_1', enter_pieces, [mid], up1, [narrow, wide, wide], 'gather', w_down[1], 3)
        up1_again = again(w_up[1], s1)
        part = grad(s1, grad_out)
        da1, x_out, grad_down1 = fused_call(
            'back_hidden_1', back_hidden_leave_pieces, [grad_out, a1, s1, mid], down1, [wide, narrow], 'scatter', part, 4)
        down0_again = again(w_down[0], da1)
        up0_again = again(w_up[0], da1)
        part = grad(u1, da1)
        du_scratch = [pltpu.VMEM((t // STEPS, d), F32)]
        d_mid, grad_up1 = fused_call('back_input_1', back_input_pieces, [da1, mid, grad_out], up1_again, [narrow], 'scatter', part, 5, du_scratch)
        part = grad(s0, d_mid)
        da0, grad_down0 = fused_call('back_hidden_0', back_hidden_pieces, [d_mid, a0], down0_again, [wide], 'scatter', part, 6)
        part = grad(u0, da0)
        dx_in, grad_up0 = fused_call('back_input_0', back_input_pieces, [da0, tokens, d_mid], up0_again, [narrow], 'scatter', part, 7, du_scratch)
        return x_out, dx_in, jnp.stack([grad_up0, grad_up1]), jnp.stack([grad_down0, grad_down1])

    return jax.shard_map(device_fn, mesh=mesh, in_specs=(tok_spec, tok_spec, w_spec, w_spec), out_specs=(tok_spec, tok_spec, w_spec, w_spec), check_vma=False)
```

time: 1690 us -> 850 us (0.50)
  waiting for transfers between devices: 1260 us -> 0.55 us
  Pallas kernels: 0 us -> 716 us
  matrix products: 345 us -> 95.6 us
  local copies, waits for them, and re-layouts: 43.2 us -> 9.35 us
    pallas_call x0 -> x8, Pallas kernels: none -> 716 us  [the longest x7 656 us: fused_call(): pl.pallas_call(kernel, grid=(STEPS,), out_shape=out_shape, in_specs=[row_...]
    reduce_scatter x4 -> x0, waiting for transfers between devices: 701 us -> none  [the longest x2 371 us: device_fn(): lax.psum_scatter(down_part, BOTH_AXES, scatter_dimension=0, tiled=True)]
    all_gather x8 -> x3, waiting for transfers between devices: 560 us -> 0.01 us  [again(): return lax.all_gather(shard, BOTH_AXES, axis=0, tiled=True)]
    dot_general x12 -> x4, matrix products: 345 us -> 95.6 us  [grad(): part = lax.dot_general(lhs, rhs, CONTRACT_ROWS, preferred_element_type=F32)]
    unnamed x32 -> x12, local copies, waits for them, and re-layouts: 27 us -> 6.67 us
  transfers between devices with their start and end apart: 12 -> 3, of which waited for: 11 -> 0; matrix products, arithmetic and copies ran while one was open for 24% -> 11% of each run, Pallas kernels for 0% -> 41%
where the time goes in v1:
time: 850 us; the launch traced here: 840 us
  Pallas kernels  716 us (84%)
  matrix products  95.6 us (11%)
  between operations  14.3 us (2%)
  local copies, waits for them, and re-layouts  9.35 us (1%)
    pallas_call x7, Pallas kernels, fused_call(): pl.pallas_call(kernel, grid=(STEPS,), out_shape=out_shape, in_specs=[row_...  656 us
    dot_general x4, matrix products, grad(): part = lax.dot_general(lhs, rhs, CONTRACT_ROWS, preferred_element_type=F32)  95.6 us
    pallas_call x1, Pallas kernels, gather_alone(): pl.pallas_call(kernel, out_shape=jax.ShapeDtypeStruct((4, 8, n, m), shard...  60.1 us
  transfers between devices with their start and end apart: 3, of which 0 were waited for; matrix products, arithmetic and copies ran while one was open for 11% of the time, Pallas kernels for 41%

profile of v1, /device:TPU:14, one launch (start us, length us, event | category | flops | bytes accessed | tf_op | source)
XLA Modules:
  0.0 840.4 jit_solution(8103383786624515253)
XLA Ops:
  7.2 0.0 all-gather.4.cloned.1.call-start
  7.2 1.9 slice_bitcast_fusion.1
  9.1 0.0 copy-start.1
  9.1 60.1 %gather_alone.1 = bf16[4,8,32,4096]{3,2,1,0:T(8,128)(2,1)} custom-call(bf16[32,4096]{1,0:T(8,128)(2,1)} %get-tuple-element.41.shard_ref), custom_call_target="tpu_custom_call" | custom-call | flops 17179869184 | bytes 16777216 | tf_op jit(solution)/shard_map/gather_alone/pallas_call | solution.py:429
  69.2 0.0 copy-done.1
  69.2 0.8 slice_bitcast_fusion
  70.0 72.4 %enter_0.1 = (bf16[2048,1024]{1,0:T(8,128)(2,1)}, bf16[2048,4096]{1,0:T(8,128)(2,1)}, bf16[2048,4096]{1,0:T(8,128)(2,1)}, bf16[4,8,128,1024]{3,2,1,0:T(8,128)(2,1)}) custom-call(bf16[2048,1024]{1,0:T(8,128)(2,1)} %refs_1_.3, bf16[1024,4096]{1,0:T(8,128)(2,1)} %bitcast.38, bf16[128,1024]{1,0:T(8,128)(2,1)} %get-tuple-element.39.refs_2_), custom_call_target="tpu_custom_call" | custom-call | flops 34359738368 | bytes 67108864 | tf_op jit(solution)/shard_map/enter_0/pallas_call | solution.py:405
  142.4 67.1 %leave_0.1 = (bf16[2048,1024]{1,0:T(8,128)(2,1)}, bf16[4,8,32,4096]{3,2,1,0:T(8,128)(2,1)}) custom-call(bf16[2048,4096]{1,0:T(8,128)(2,1)} %get-tuple-element.26.refs_0_, bf16[2048,1024]{1,0:T(8,128)(2,1)} %refs_1_.3, bf16[4096,1024]{1,0:T(8,128)(2,1)} %bitcast.37, bf16[32,4096]{1,0:T(8,128)(2,1)} %get-tuple-element.35.refs_3_), custom_call_target="tpu_custom_call" | custom-call | flops 34359738368 | bytes 67108864 | tf_op jit(solution)/shard_map/leave_0/pallas_call | solution.py:405
  209.5 72.4 %enter_1.1 = (bf16[2048,1024]{1,0:T(8,128)(2,1)}, bf16[2048,4096]{1,0:T(8,128)(2,1)}, bf16[2048,4096]{1,0:T(8,128)(2,1)}, bf16[4,8,128,1024]{3,2,1,0:T(8,128)(2,1)}) custom-call(bf16[2048,1024]{1,0:T(8,128)(2,1)} %get-tuple-element.28.refs_0_.refs_3_.refs_1_, bf16[1024,4096]{1,0:T(8,128)(2,1)} %bitcast.39, bf16[128,1024]{1,0:T(8,128)(2,1)} %get-tuple-element.48.refs_2_), custom_call_target="tpu_custom_call" | custom-call | flops 34359738368 | bytes 67108864 | tf_op jit(solution)/shard_map/enter_1/pallas_call | solution.py:405
  281.9 0.0 all-gather.4.cloned.1.call-update
  281.9 0.5 all-gather.6.cloned.1.call-start
  282.4 23.8 %fusion = f32[4096,1024]{1,0:T(8,128)} fusion(bf16[2048,4096]{1,0:T(8,128)(2,1)} %get-tuple-element.31.refs_2_, bf16[2048,1024]{1,0:T(8,128)(2,1)} %refs_2_.1), kind=kOutput, calls=%fused_computation.6 | convolution fusion | flops 17179869184 | bytes 37748736 | tf_op jit(solution)/shard_map/dot_general | solution.py:456
  306.2 115.8 %back_hidden_1.1 = (bf16[2048,4096]{1,0:T(8,128)(2,1)}, bf16[2048,1024]{1,0:T(8,128)(2,1)}, f32[128,1024]{1,0:T(8,128)}) custom-call(bf16[2048,1024]{1,0:T(8,128)(2,1)} %refs_2_.1, bf16[2048,4096]{1,0:T(8,128)(2,1)} %get-tuple-element.30.refs_1_, bf16[2048,4096]{1,0:T(8,128)(2,1)} %get-tuple-element.31.refs_2_, ...), custom_call_target="tpu_custom_call" | custom-call | flops 34359738368 | bytes 67108864 | tf_op jit(solution)/shard_map/back_hidden_1/pallas_call | solution.py:405
  422.1 0.0 all-gather.6.cloned.1.call-update
  422.1 0.2 all-gather.8.cloned.1.call-start
  422.3 0.5 all-gather.8.cloned.1.call-update
  422.8 23.8 %fusion.1 = f32[1024,4096]{1,0:T(8,128)} fusion(bf16[2048,1024]{1,0:T(8,128)(2,1)} %get-tuple-element.36, bf16[2048,4096]{1,0:T(8,128)(2,1)} %get-tuple-element.34.refs_0_), kind=kOutput, calls=%fused_computation.7 | convolution fusion | flops 17179869184 | bytes 37748736 | tf_op jit(solution)/shard_map/dot_general | solution.py:456
  446.6 131.9 %back_input_1.1 = (bf16[2048,1024]{1,0:T(8,128)(2,1)}, f32[32,4096]{1,0:T(8,128)}) custom-call(bf16[2048,4096]{1,0:T(8,128)(2,1)} %get-tuple-element.34.refs_0_, bf16[2048,1024]{1,0:T(8,128)(2,1)} %get-tuple-element.28.refs_0_.refs_3_.refs_1_, bf16[2048,1024]{1,0:T(8,128)(2,1)} %refs_2_.1, bf16[1024,4096]{1,0:T(8,128)(2,1)} %all-gather.4.cloned.1.call-done.refs_3_, ...), custom_call_target="tpu_custom_call" | custom-call | flops 34359738368 | bytes 67108864 | tf_op jit(solution)/shard_map/back_input_1/pallas_call | solution.py:405
  578.5 24.0 %fusion.2 = f32[4096,1024]{1,0:T(8,128)} fusion(bf16[2048,4096]{1,0:T(8,128)(2,1)} %get-tuple-element.26.refs_0_, bf16[2048,1024]{1,0:T(8,128)(2,1)} %get-tuple-element.37.refs_0_.refs_2_), kind=kOutput, calls=%fused_computation.8 | convolution fusion | flops 17179869184 | bytes 37748736 | tf_op jit(solution)/shard_map/dot_general | solution.py:456
  602.5 97.3 %back_hidden_0.1 = (bf16[2048,4096]{1,0:T(8,128)(2,1)}, f32[128,1024]{1,0:T(8,128)}) custom-call(bf16[2048,1024]{1,0:T(8,128)(2,1)} %get-tuple-element.37.refs_0_.refs_2_, bf16[2048,4096]{1,0:T(8,128)(2,1)} %get-tuple-element.38.refs_1_, bf16[4096,1024]{1,0:T(8,128)(2,1)} %all-gather.6.cloned.1.call-done.refs_2_, f32[4,8,128,1024]{3,2,1,0:T(8,128)} %bitcast.34), custom_call_target="tpu_custom_call" | custom-call | flops 34359738368 | bytes 67108864 | tf_op jit(solution)/shard_map/back_hidden_0/pallas_call | solution.py:405
  699.9 24.0 %fusion.3 = f32[1024,4096]{1,0:T(8,128)} fusion(bf16[2048,1024]{1,0:T(8,128)(2,1)} %get-tuple-element.42, bf16[2048,4096]{1,0:T(8,128)(2,1)} %get-tuple-element.40.refs_0_), kind=kOutput, calls=%fused_computation.9 | convolution fusion | flops 17179869184 | bytes 37748736 | tf_op jit(solution)/shard_map/dot_general | solution.py:456
  723.9 0.0 copy-start.3
  724.0 99.0 %back_input_0.1 = (bf16[2048,1024]{1,0:T(8,128)(2,1)}, f32[32,4096]{1,0:T(8,128)}) custom-call(bf16[2048,4096]{1,0:T(8,128)(2,1)} %get-tuple-element.40.refs_0_, bf16[2048,1024]{1,0:T(8,128)(2,1)} %refs_1_.3, bf16[2048,1024]{1,0:T(8,128)(2,1)} %get-tuple-element.37.refs_0_.refs_2_, bf16[1024,4096]{1,0:T(8,128)(2,1)} %all-gather.8.cloned.1.call-done.refs_3_, ...), custom_call_target="tpu_custom_call" | custom-call | flops 34359738368 | bytes 67108864 | tf_op jit(solution)/shard_map/back_input_0/pallas_call | solution.py:405
  823.0 0.0 copy-start
  823.0 0.0 copy-done.2
  823.0 0.0 copy-done.4
  823.0 1.1 pad_maximum_fusion.1
  824.1 0.0 copy-done.3
  824.1 2.6 pad_maximum_fusion
  826.7 4.6 copy.10
  831.4 0.0 copy-done
  831.4 2.0 copy.11
  (5 shorter events, 0.0 us)
Async XLA Ops:
  7.2 439.5 %all-gather.4.cloned.1.call-start = ((), (), s32[]{:S(2)}) async-start(), calls=%async_computation | async-start | bytes 8650752 | tf_op jit(solution)/shard_map/all_gather | solution.py:453
  9.1 60.1 %copy-start.1 = (bf16[2,128,1024]{2,1,0:T(8,128)(2,1)S(1)}, bf16[2,128,1024]{2,1,0:T(8,128)(2,1)}, u32[]{:S(2)}) copy-start(bf16[2,128,1024]{2,1,0:T(8,128)(2,1)} %param.7) | copy-start | bytes 1572868
  281.9 320.6 %all-gather.6.cloned.1.call-start = ((), (), s32[]{:S(2)}) async-start(), calls=%async_computation.1 | async-start | bytes 8650752 | tf_op jit(solution)/shard_map/all_gather | solution.py:453
  422.1 301.8 %all-gather.8.cloned.1.call-start = ((), (), s32[]{:S(2)}) async-start(), calls=%async_computation.2 | async-start | bytes 8650752 | tf_op jit(solution)/shard_map/all_gather | solution.py:453
  723.9 99.1 %copy-start.2 = (f32[128,1024]{1,0:T(8,128)S(1)}, f32[128,1024]{1,0:T(8,128)}, u32[]{:S(2)}) copy-start(f32[128,1024]{1,0:T(8,128)} %get-tuple-element.47) | copy-start | bytes 1572868
  723.9 99.1 %copy-start.4 = (f32[128,1024]{1,0:T(8,128)S(1)}, f32[128,1024]{1,0:T(8,128)}, u32[]{:S(2)}) copy-start(f32[128,1024]{1,0:T(8,128)} %get-tuple-element.46) | copy-start | bytes 1572868
  723.9 100.2 %copy-start.3 = (f32[32,4096]{1,0:T(8,128)S(1)}, f32[32,4096]{1,0:T(8,128)}, u32[]{:S(2)}) copy-start(f32[32,4096]{1,0:T(8,128)} %get-tuple-element.45) | copy-start | bytes 1572868
  823.0 8.4 copy-start
Sparse Core Ops, SparseCore 0:
  282.0 94.0 all-gather.3
  422.2 92.1 all-gather.5
  517.9 88.5 all-gather.7
